TPU v7x, 32 devices: a whole 2x2x4 slice. The times are simulated.
32 devices in a mesh: replica: 2 (over x), pipe: 4 (over z), tensor: 4 (over y, core).
Axes of the slice: x: 2, y: 2, z: 4, core: 2. Of those that a mesh axis runs over, the one named last changes fastest.
Arguments:
- queries: bfloat16 [256, 8192], P('replica', ('pipe', 'tensor')), parts along dimension 0, may hold values from -128 to 128, as said below
- cache_keys: bfloat16 [8, 4096, 1024], P('replica', 'tensor', 'pipe'), parts along dimension 0, may hold values from -4 to 4
- cache_values: bfloat16 [8, 4096, 1024], P('replica', 'tensor', 'pipe'), parts along dimension 0, may hold values from -6 to 6
- prefix_lengths: int32 [8], P('replica'), parts along dimension 0, may hold values from 2048 to 4064
- residual_in: bfloat16 [256, 8192], P('replica', ('pipe', 'tensor')), parts along dimension 0, may hold values from -64 to 64
- out_weight: bfloat16 [8192, 4, 2048], P('pipe', None, 'tensor'), may hold values from -0.0625 to 0.0625
- norm_gain: float32 [8192], P(('pipe', 'tensor')), may hold values from 0.1 to 1.9
Outputs:
- residual_out: bfloat16 [256, 8192], P('replica', ('pipe', 'tensor')), parts along dimension 0
- normed: bfloat16 [256, 8192], P('replica', ('pipe', 'tensor')), parts along dimension 0
There are 2 independent parts, one for each index of `replica`. A program takes and returns all parts, laid end to end along the dimension named above; an argument that names none is the same for every part. Nothing has to cross between parts.
Inputs may be any that keep to these rules, and one draw needn't show every extreme that they name: `queries`: entries of the query rows; some rows may be much longer than others. The span's own keys and values already stand in the cache, in slots prefix_lengths[r] to prefix_lengths[r] + 31; later slots hold unused entries.
All inputs are finite; a program needn't handle non-finite values.
Results may differ from a plain program's by a relative error of at most 0.018.
Values may be sent and summed in bfloat16 or wider, within the bound.
A program may use at most 64 MiB of HBM per device.

v0:
```python
import math

import jax
import jax.numpy as jnp
from jax import lax
from jax.sharding import PartitionSpec as P

D = 8192
HD = 128


masked_value = -1e30
epsilon = 1e-05


def combined_all(shard, axis, combine):
    everything = jax.tree.map(
        lambda part, kind: lax.all_gather(part.astype(kind), axis),
        shard,
        (jnp.bfloat16, jnp.bfloat16, jnp.bfloat16),
    )

    def take(k):
        return jax.tree.map(lambda part, own: part[k].astype(own.dtype), everything, shard)

    return lax.fori_loop(
        1, lax.axis_size(axis), lambda k, so_far: combine(so_far, take(k)), take(0)
    )


def combine(first, second):
    peak_one, total_one, summed_one = first
    peak_two, total_two, summed_two = second
    joined = jnp.maximum(peak_one, peak_two)
    factor_one = jnp.exp(peak_one - joined)
    factor_two = jnp.exp(peak_two - joined)
    return (
        joined,
        total_one * factor_one + total_two * factor_two,
        summed_one * factor_one[..., None] + summed_two * factor_two[..., None],
    )


def on_device(
    queries, cache_keys, cache_values, prefix_lengths, residual_in, out_weight, norm_gain
):
    tok_rows = queries.shape[0]
    requests = prefix_lengths.shape[0]
    span_len = tok_rows // requests
    slot_count = cache_keys.shape[1]
    local_groups = cache_keys.shape[2] // HD
    gathered = lax.all_gather(queries, "tensor", axis=1, tiled=True)
    heads_here = gathered.shape[1] // HD
    group_size = heads_here // local_groups
    queries_here = gathered.reshape(requests, span_len, local_groups, group_size, HD)
    keys_here = cache_keys.reshape(requests, slot_count, local_groups, HD)
    values_here = cache_values.reshape(requests, slot_count, local_groups, HD)
    scores = jnp.einsum(
        "rcghd,rjgd->rcghj", queries_here, keys_here, preferred_element_type=jnp.float32
    ) * (1.0 / math.sqrt(HD))
    first_slot = lax.axis_index("tensor") * slot_count
    slot_index = first_slot + jnp.arange(slot_count, dtype=jnp.int32)
    limits = prefix_lengths[:, None] + jnp.arange(span_len, dtype=jnp.int32)[None, :]
    visible = (slot_index[None, None, :] <= limits[:, :, None])[:, :, None, None, :]
    masked = jnp.where(visible, scores, masked_value)
    row_peak = jnp.max(masked, axis=-1)
    weights = jnp.where(visible, jnp.exp(masked - row_peak[..., None]), 0.0)
    row_total = jnp.sum(weights, axis=-1)
    weighted = jnp.einsum(
        "rcghj,rjgd->rcghd",
        weights.astype(jnp.bfloat16),
        values_here,
        preferred_element_type=jnp.float32,
    )
    row_peak = row_peak.reshape(tok_rows, heads_here)
    row_total = row_total.reshape(tok_rows, heads_here)
    weighted = weighted.reshape(tok_rows, heads_here, HD)
    row_peak, row_total, weighted = combined_all((row_peak, row_total, weighted), "tensor", combine)
    attended = (
        (weighted / row_total[..., None]).astype(jnp.bfloat16).reshape(tok_rows, heads_here * HD)
    )
    col_groups = out_weight.shape[1]
    col_width = out_weight.shape[2]
    partial_value = jnp.dot(
        attended,
        out_weight.reshape(out_weight.shape[0], col_groups * col_width),
        preferred_element_type=jnp.float32,
    )
    projected = (
        lax.psum_scatter(
            partial_value.reshape(tok_rows, col_groups, col_width).astype(jnp.bfloat16),
            "pipe",
            scatter_dimension=1,
            tiled=True,
        )
        .astype(jnp.float32)
        .reshape(tok_rows, col_width)
    )
    updated = residual_in.astype(jnp.float32) + projected
    squares = lax.psum(jnp.sum(updated * updated, axis=1), ("pipe", "tensor"))
    normed = updated * lax.rsqrt(squares / D + epsilon)[:, None] * norm_gain[None, :]
    return (updated.astype(jnp.bfloat16), normed.astype(jnp.bfloat16))


def solution(mesh):
    in_specs = (
        P("replica", ("pipe", "tensor")),
        P("replica", "tensor", "pipe"),
        P("replica", "tensor", "pipe"),
        P("replica"),
        P("replica", ("pipe", "tensor")),
        P("pipe", None, "tensor"),
        P(("pipe", "tensor")),
    )
    out_specs = (P("replica", ("pipe", "tensor")), P("replica", ("pipe", "tensor")))
    return jax.shard_map(
        on_device, mesh=mesh, in_specs=in_specs, out_specs=out_specs, check_vma=False
    )
```

profile of v0, /device:TPU:0, one launch (start us, length us, event | category | flops | bytes accessed | tf_op | source)
XLA Modules:
  0.0 146.8 jit_solution(17740853063644884456)
XLA Ops:
  7.2 0.7 iota_add_fusion.1
  7.9 8.9 %all_gather.15 = bf16[128,2048]{1,0:T(8,128)(2,1)S(1)} all-gather(bf16[128,512]{1,0:T(8,128)(2,1)} %param.9), channel_id=1, replica_groups=mesh['replica'=2,'pipe'=4,'tensor'=4] {'tensor'}, dimensions={1}, use_global_device_ids=true | all-gather | bytes 655360 | tf_op jit(solution)/shard_map/all_gather | solution.py:52
  16.8 0.1 copy.52
  16.9 4.0 %reshape.107 = bf16[4,1024,2,128]{3,2,1,0:T(2,128)(2,1)} reshape(bf16[4,1024,256]{2,1,0:T(8,128)(2,1)} %param.10) | data formatting | bytes 4194304 | tf_op jit(solution)/shard_map/reshape | solution.py:56
  20.9 2.5 %reshape.109 = bf16[4,1024,2,128]{3,2,1,0:T(2,128)(2,1)S(1)} reshape(bf16[4,1024,256]{2,1,0:T(8,128)(2,1)} %param.11) | data formatting | bytes 4194304 | tf_op jit(solution)/shard_map/reshape | solution.py:57
  23.5 0.1 broadcast_compare_fusion
  23.6 3.3 %fusion.3 = (f32[4,32,2,8]{1,3,2,0:T(8,128)S(1)}, f32[4,2,1024,32,8]{2,3,4,1,0:T(8,128)S(1)}) fusion(pred[4,32,1024]{2,1,0:T(8,128)(4,1)S(1)} %broadcast_compare_fusion, bf16[4,32,2,8,128]{4,3,2,1,0:T(8,128)(2,1)S(1)} %bitcast.77, bf16[4,1024,2,128,1]{3,2,1,0,4:T(2,128)(2,1)} %bitcast.75), kind=kOutput, calls=%fused_computation.10 | convolution fusion | flops 543160320 | bytes 11149312 | tf_op jit(solution)/shard_map/rcghd,rjgd->rcghj/dot_general | solution.py:58
  26.9 2.6 %fusion.17 = bf16[4,32,2,8,128]{4,1,3,2,0:T(8,128)(2,1)S(1)} fusion(bf16[4,1024,2,128,1]{3,2,1,0,4:T(2,128)(2,1)S(1)} %bitcast.74, f32[4,2,1024,32,8]{2,3,4,1,0:T(8,128)S(1)} %get-tuple-element.202, f32[4,32,2,8]{1,3,2,0:T(8,128)S(1)} %get-tuple-element.201, pred[4,32,1024]{2,1,0:T(8,128)(4,1)S(1)} %broadcast_compare_fusion), kind=kOutput, calls=%fused_computation.20 | convolution fusion | flops 547618816 | bytes 11149312 | tf_op jit(solution)/shard_map/rcghj,rjgd->rcghd/dot_general | solution.py:69
  29.5 0.6 copy-done
  30.1 1.0 copy.43
  31.3 4.7 %fusion.5 = bf16[4,32,2,8]{1,3,2,0:T(8,128)(2,1)S(1)} fusion(f32[4,2,1024,32,8]{2,3,4,1,0:T(8,128)} %copy-done, f32[4,32,2,8]{1,3,2,0:T(8,128)S(1)} %get-tuple-element.201, pred[4,32,1024]{2,1,0:T(8,128)(4,1)S(1)} %broadcast_compare_fusion), kind=kLoop, calls=%fused_computation.12 | loop fusion | flops 10483712 | bytes 8531968 | tf_op jit(solution)/shard_map/reduce_sum | solution.py:68
  36.1 10.5 %copy.53 = bf16[256,8,4,512]{3,1,2,0:T(8,128)(2,1)} copy(bf16[256,8,4,512]{3,2,1,0:T(4,128)(2,1)} %bitcast.72) | data formatting | bytes 16777216
  46.6 12.3 %copy.45 = bf16[2048,2048]{1,0:T(8,128)(2,1)} copy(bf16[2048,2048]{0,1:T(8,128)(2,1)} %bitcast.71) | data formatting | bytes 16777216 | tf_op jit(solution)/shard_map/dot_general | solution.py:84
  59.0 5.2 %all_gather.17 = bf16[4,128,16]{1,2,0:T(8,128)(2,1)S(1)} all-gather(bf16[1,128,16]{1,2,0:T(8,128)(2,1)S(1)} %convert_element_type.124), channel_id=1, replica_groups=mesh['replica'=2,'pipe'=4,'tensor'=4] {'tensor'}, dimensions={0}, use_global_device_ids=true | all-gather | bytes 20480 | tf_op jit(solution)/shard_map/all_gather | solution.py:18
  64.2 5.4 %all_gather.16 = bf16[4,128,16]{1,2,0:T(8,128)(2,1)S(1)} all-gather(bf16[1,128,16]{1,2,0:T(8,128)(2,1)S(1)} %convert_element_type.120), channel_id=1, replica_groups=mesh['replica'=2,'pipe'=4,'tensor'=4] {'tensor'}, dimensions={0}, use_global_device_ids=true | all-gather | bytes 20480 | tf_op jit(solution)/shard_map/all_gather | solution.py:18
  69.6 1.1 fusion.22
  70.7 6.5 %while.19 = (s32[]{:T(128)}, f32[128,16]{0,1:T(8,128)S(1)}, f32[128,16]{0,1:T(8,128)S(1)}, f32[128,16,128]{2,1,0:T(8,128)S(1)}, bf16[4,128,16]{1,2,0:T(8,128)(2,...) while((s32[]{:T(128)}, f32[128,16]{0,1:T(8,128)S(1)}, ...), condition=%wide.region_3.4_spmd, body=%wide.region_2.3_spmd.sunk | while | flops 1064965 | bytes 2728079 | solution.py:26
  70.7 0.1 copy.70
  70.8 0.1 copy.71
  70.9 1.9 %fusion.36 = f32[128,16,128]{2,1,0:T(8,128)S(1)} fusion(f32[128,16,128]{2,1,0:T(8,128)S(1)} %get-tuple-element.267, f32[128,16]{1,0:T(8,128)S(1)} %copy.70, bf16[4,128,16,128]{3,2,1,0:T(8,128)(2,1)} %get-tuple-element.280, s32[]{:T(128)S(6)} %select_n.46, f32[128,16]{1,0:T(8,128)S(1)} %copy.71), kind=kLoop, calls=%fused_computation.1.clone.1 | loop fusion | flops 1048576 | bytes 2637828 | tf_op jit(solution)/shard_map/while/body/eval_jaxpr/add | solution.py:40
  72.9 0.1 copy.70
  73.1 1.9 %fusion.36 = f32[128,16,128]{2,1,0:T(8,128)S(1)} fusion(f32[128,16,128]{2,1,0:T(8,128)S(1)} %get-tuple-element.267, f32[128,16]{1,0:T(8,128)S(1)} %copy.70, bf16[4,128,16,128]{3,2,1,0:T(8,128)(2,1)} %get-tuple-element.280, s32[]{:T(128)S(6)} %select_n.46, f32[128,16]{1,0:T(8,128)S(1)} %copy.71), kind=kLoop, calls=%fused_computation.1.clone.1 | loop fusion | flops 1048576 | bytes 2637828 | tf_op jit(solution)/shard_map/while/body/eval_jaxpr/add | solution.py:40
  75.1 0.1 copy.70
  75.3 1.9 %fusion.36 = f32[128,16,128]{2,1,0:T(8,128)S(1)} fusion(f32[128,16,128]{2,1,0:T(8,128)S(1)} %get-tuple-element.267, f32[128,16]{1,0:T(8,128)S(1)} %copy.70, bf16[4,128,16,128]{3,2,1,0:T(8,128)(2,1)} %get-tuple-element.280, s32[]{:T(128)S(6)} %select_n.46, f32[128,16]{1,0:T(8,128)S(1)} %copy.71), kind=kLoop, calls=%fused_computation.1.clone.1 | loop fusion | flops 1048576 | bytes 2637828 | tf_op jit(solution)/shard_map/while/body/eval_jaxpr/add | solution.py:40
  77.3 0.1 copy.44
  77.4 0.3 divide_convert_fusion
  77.7 0.2 reshape.124
  77.9 7.1 %convolution_convert_fusion = bf16[128,4,512]{2,0,1:T(8,128)(2,1)} fusion(bf16[128,2048,1]{1,0,2:T(8,128)(2,1)S(1)} %reshape.124, bf16[4,512,2048]{2,1,0:T(8,128)(2,1)} %bitcast.70), kind=kOutput, calls=%fused_computation.19 | convolution fusion | flops 1074003968 | bytes 9437184 | tf_op jit(solution)/shard_map/dot_general | solution.py:84
  85.1 22.6 %reduce-scatter.2.cloned.1.call-done = bf16[128,1,512]{2,0,1:T(8,128)(2,1)} async-done(((bf16[128,4,512]{2,0,1:T(8,128)(2,1)}), bf16[128,1,512]{2,0,1:T(8,128)(2,1)}) %reduce-scatter.2.cloned.1.call-update) | async-done | bytes 131088 | tf_op jit(solution)/shard_map/reduce_scatter | solution.py:90
  107.7 1.0 multiply_reduce_fusion
  108.8 29.5 %psum.7 = f32[128]{0:T(128)S(1)} all-reduce(f32[128]{0:T(128)S(1)} %multiply_reduce_fusion), channel_id=1, replica_groups=mesh['replica'=2,'pipe'=4,'tensor'=4] {'pipe','tensor'}, use_global_device_ids=true, to_apply=%region_6.7 | all-reduce | flops 128 | bytes 1024 | tf_op jit(solution)/shard_map/psum | solution.py:100
  138.3 1.7 %multiply_convert_fusion = (bf16[128,512]{1,0:T(8,128)(2,1)}, bf16[128,512]{1,0:T(8,128)(2,1)}) fusion(bf16[128,512]{1,0:T(8,128)(2,1)S(1)} %copy-done.1, bf16[128,1,512]{2,0,1:T(8,128)(2,1)} %reduce-scatter.2.cloned.1.call-done, f32[512]{0:T(512)S(1)} %copy-done.2, f32[128]{0:T(128)S(1)} %add_rsqrt_fusion), kind=kLoop, calls=%fused_computation.26 | loop fusion | flops 458752 | bytes 526848 | tf_op jit(solution)/shard_map/convert_element_type | solution.py:102
  (24 shorter events, 0.6 us)
Async XLA Ops:
  7.2 62.4 %all-gather.2.cloned.1.call-start = ((), (), s32[]{:S(2)}) async-start(), calls=%async_computation.1 | async-start | bytes 2621440 | tf_op jit(solution)/shard_map/all_gather | solution.py:18
  26.9 3.2 %copy-start = (f32[4,2,1024,32,8]{2,3,4,1,0:T(8,128)}, f32[4,2,1024,32,8]{2,3,4,1,0:T(8,128)S(1)}, u32[]{:S(2)}) copy-start(f32[4,2,1024,32,8]{2,3,4,1,0:T(8,128)S(1)} %get-tuple-element.202) | copy-start | bytes 25165828
  31.1 76.6 %reduce-scatter.2.cloned.1.call-start = ((), (), s32[]{:S(2)}) async-start(), calls=%async_computation.2 | async-start | bytes 655360 | tf_op jit(solution)/shard_map/reduce_scatter | solution.py:90
  77.2 30.5 %copy-start.1 = (bf16[128,512]{1,0:T(8,128)(2,1)S(1)}, bf16[128,512]{1,0:T(8,128)(2,1)}, u32[]{:S(2)}) copy-start(bf16[128,512]{1,0:T(8,128)(2,1)} %param.13) | copy-start | bytes 393220
  77.2 61.0 %copy-start.2 = (f32[512]{0:T(512)S(1)}, f32[512]{0:T(512)}, u32[]{:S(2)}) copy-start(f32[512]{0:T(512)} %param.15) | copy-start | bytes 6148
Sparse Core Ops, SparseCore 0:
  31.2 23.3 all-gather.1
  85.2 22.4 reduce-scatter.1
where the time goes:
time: 148 us; the launch traced here: 147 us
  blocking collectives  48.9 us (33%)
  local copies, waits for them, and re-layouts  32.2 us (22%)
  waiting for transfers between devices  22.7 us (15%)
  other arithmetic  15.6 us (11%)
  between operations  14.2 us (10%)
  matrix products  13 us (9%)
    psum x1, blocking collectives, on_device(): squares = lax.psum(jnp.sum(updated * updated, axis=1), ('pipe', 'tensor'))  29.5 us
    reduce_scatter x1, waiting for transfers between devices, on_device(): lax.psum_scatter(partial_value.reshape(tok_rows, col_groups, col_width).a...  22.6 us
    dot_general x1, local copies, waits for them, and re-layouts, on_device(): jnp.dot(attended, out_weight.reshape(out_weight.shape[0], col_groups * co...  12.3 us
    unnamed x8, local copies, waits for them, and re-layouts  11.2 us
    all_gather x2, blocking collectives, combined_all(): lax.all_gather(part.astype(kind), axis)  10.6 us
    all_gather x1, blocking collectives, on_device(): gathered = lax.all_gather(queries, 'tensor', axis=1, tiled=True)  8.87 us
    dot_general x1, matrix products, on_device(): jnp.dot(attended, out_weight.reshape(out_weight.shape[0], col_groups * co...  7.12 us
    add x3, other arithmetic, combine(): summed_one * factor_one[..., None] + summed_two * factor_two[..., None]  5.79 us
  transfers between devices with their start and end apart: 2, of which 1 were waited for; matrix products, arithmetic and copies ran while one was open for 19% of the time, Pallas kernels for 0%

commit v1 on v0

v1 whole, which is shorter than its diff:
```python
import functools
import math

import jax
import jax.numpy as jnp
from jax import lax
from jax.experimental import pallas as pl
from jax.experimental.pallas import tpu as pltpu
from jax.sharding import PartitionSpec as P

HD = 128
LANES = 128
masked_value = -1e30
lowest_peak = -1e29
epsilon = 1e-05
MESH = pl.DeviceIdType.MESH


def kernel(
    n_pipe,
    n_tensor,
    requests,
    prefix_ref,
    q_hbm,
    k_hbm,
    v_hbm,
    w_hbm,
    res_ref,
    gain_ref,
    residual_out,
    normed_out,
    q_all,
    keys,
    values,
    w_raw,
    w_ready,
    o_send,
    st_send,
    o_recv,
    st_recv,
    att,
    acc,
    p_send,
    p_recv,
    sq_send,
    sq_recv,
    q_local_sem,
    kv_sem,
    w_sem,
    q_send_sem,
    q_recv_sem,
    o_sems,
    st_sems,
    att_send_sem,
    att_recv_sem,
    p_sems,
    sq_sems,
):
    tokens = res_ref.shape[0]
    span = tokens // requests
    heads = q_hbm.shape[1] // HD
    rows = heads * span
    chips = n_tensor // 2
    n_groups, slots = keys.shape[1], keys.shape[2]
    group_size = n_tensor * heads // n_groups
    col_groups, depth, width = w_ready.shape
    depth_each = depth // n_tensor
    devices = n_pipe * n_tensor
    coef = math.log2(math.e) / math.sqrt(HD)

    me_p = lax.axis_index("pipe")
    me = lax.axis_index("tensor")
    chip = me // 2
    core = lax.rem(me, 2)
    partner = chip * 2 + 1 - core
    flat = me_p * n_tensor + me

    def other_chip(d):
        return lax.rem(chip + d, chips)

    def group_of(c):
        return (c * 2 * heads) // group_size

    def q_local(r, h):
        return pltpu.make_async_copy(
            q_hbm.at[pl.ds(r * span, span), pl.ds(h * HD, HD)],
            q_all.at[chip, r, pl.ds(core * rows + h * span, span)],
            q_local_sem.at[r, h],
        )

    def kv_copy(which, r, g):
        src, dst = ((k_hbm, keys), (v_hbm, values))[which]
        return pltpu.make_async_copy(
            src.at[r, :, pl.ds(pl.multiple_of(g * HD, HD), HD)], dst.at[r, g], kv_sem.at[which, r, g]
        )

    for r in range(requests):
        for h in range(heads):
            q_local(r, h).start()
    for gi in range(n_groups):
        for r in range(requests):
            g = lax.rem(group_of(chip) + gi, n_groups)
            kv_copy(0, r, g).start()
            kv_copy(1, r, g).start()
    w_copy = pltpu.make_async_copy(w_hbm, w_raw, w_sem)
    w_copy.start()

    barrier = pltpu.get_barrier_semaphore()

    def greet(i, carry):
        other = lax.rem(flat + i, devices)
        pl.semaphore_signal(
            barrier,
            inc=1,
            device_id={"pipe": other // n_tensor, "tensor": lax.rem(other, n_tensor)},
            device_id_type=MESH,
        )
        return carry

    lax.fori_loop(1, devices, greet, 0)
    pl.semaphore_wait(barrier, devices - 1)

    def q_piece(owner_chip, owner_core, r, hop, target):
        piece = q_all.at[owner_chip, r, pl.ds(owner_core * rows, rows)]
        return pltpu.make_async_remote_copy(
            src_ref=piece,
            dst_ref=piece,
            send_sem=q_send_sem.at[hop, r],
            recv_sem=q_recv_sem.at[owner_chip * 2 + owner_core, r],
            device_id={"tensor": target},
            device_id_type=MESH,
        )

    for r in range(requests):
        for h in range(heads):
            q_local(r, h).wait()
        for d in range(1, chips):
            q_piece(chip, core, r, d, other_chip(d) * 2 + core).start()
        q_piece(chip, core, r, 0, partner).start()

    def parts_to(target, r):
        return (
            pltpu.make_async_remote_copy(
                src_ref=o_send.at[target, r],
                dst_ref=o_recv.at[me, r],
                send_sem=o_sems.at[0, target, r],
                recv_sem=o_sems.at[1, me, r],
                device_id={"tensor": target},
                device_id_type=MESH,
            ),
            pltpu.make_async_remote_copy(
                src_ref=st_send.at[target, r],
                dst_ref=st_recv.at[me, r],
                send_sem=st_sems.at[0, target, r],
                recv_sem=st_sems.at[1, me, r],
                device_id={"tensor": target},
                device_id_type=MESH,
            ),
        )

    def parts_from(source, r):
        return (
            pltpu.make_async_remote_copy(
                src_ref=o_send.at[me, r],
                dst_ref=o_recv.at[source, r],
                send_sem=o_sems.at[0, source, r],
                recv_sem=o_sems.at[1, source, r],
                device_id={"tensor": partner},
                device_id_type=MESH,
            ),
            pltpu.make_async_remote_copy(
                src_ref=st_send.at[me, r],
                dst_ref=st_recv.at[source, r],
                send_sem=st_sems.at[0, source, r],
                recv_sem=st_sems.at[1, source, r],
                device_id={"tensor": partner},
                device_id_type=MESH,
            ),
        )

    joint = rows % LANES == 0
    pieces = ((0, 2 * rows),) if joint else ((0, rows), (rows, rows))

    def unit(owner_chip, r):
        g = group_of(owner_chip)
        for start, count in pieces:
            q = q_all[owner_chip, r, pl.ds(start, count), :]
            s = lax.dot_general(
                keys[r, g], q, (((1,), (1,)), ((), ())), preferred_element_type=jnp.float32
            )
            slot = me * slots + lax.broadcasted_iota(jnp.int32, (slots, count), 0)
            token = lax.rem(lax.broadcasted_iota(jnp.int32, (1, count), 1), span)
            s = jnp.where(slot <= prefix_ref[r] + token, s, masked_value)
            peak = jnp.maximum(jnp.max(s, axis=0, keepdims=True), lowest_peak)
            p = jnp.exp2((s - peak) * coef)
            total = jnp.sum(p, axis=0, keepdims=True)
            o = lax.dot_general(
                values[r, g],
                p.astype(jnp.bfloat16),
                (((0,), (0,)), ((), ())),
                preferred_element_type=jnp.float32,
            )
            row = lax.broadcasted_iota(jnp.int32, (8, count), 0)
            stats = jnp.where(row < 4, peak, total)
            for k in range(count // rows):
                target = owner_chip * 2 + start // rows + k
                o_send[target, r] = o[:, k * rows : (k + 1) * rows].astype(jnp.bfloat16)
                st_send[target, r] = stats[:, k * rows : (k + 1) * rows]

    def own_unit(r, carry):
        g = group_of(chip)
        kv_copy(0, r, g).wait()
        kv_copy(1, r, g).wait()
        q_piece(chip, 1 - core, r, 0, partner).wait_recv()
        unit(chip, r)
        for copy in parts_to(partner, r):
            copy.start()
        for d in range(1, chips):
            q_piece(other_chip(d), core, r, 0, partner).wait_recv()
            q_piece(other_chip(d), core, r, chips - 1 + d, partner).start()
        return carry

    lax.fori_loop(0, requests, own_unit, 0)

    for gi in range(1, n_groups):
        for r in range(requests):
            g = lax.rem(group_of(chip) + gi, n_groups)
            kv_copy(0, r, g).wait()
            kv_copy(1, r, g).wait()

    def far_unit(i, carry):
        c = other_chip(1 + i // requests)
        r = lax.rem(i, requests)
        q_piece(c, 1 - core, r, 0, partner).wait_recv()
        unit(c, r)
        for k in range(2):
            for copy in parts_to(c * 2 + k, r):
                copy.start()
        return carry

    lax.fori_loop(0, (chips - 1) * requests, far_unit, 0)

    w_copy.wait()
    lane_blocks = width // LANES
    per_depth = lane_blocks * col_groups
    block = 16 * per_depth
    to_row = lax.broadcasted_iota(jnp.int32, (block, block), 0)
    from_row = lax.broadcasted_iota(jnp.int32, (block, block), 1)
    order = jnp.where(
        from_row == lax.rem(to_row, 16) * per_depth + to_row // 16, 1.0, 0.0
    ).astype(jnp.bfloat16)

    def reorder(i, carry):
        pair = jnp.concatenate(
            [w_raw[pl.ds((2 * i + k) * block, block), :] for k in range(2)], axis=1
        )
        ordered = jnp.dot(order, pair, preferred_element_type=jnp.float32).astype(jnp.bfloat16)
        for j in range(lane_blocks):
            for g in range(col_groups):
                at = (j * col_groups + g) * 16
                for k in range(2):
                    w_ready[g, pl.ds((2 * i + k) * 16, 16), j * LANES : (j + 1) * LANES] = ordered[
                        at : at + 16, k * LANES : (k + 1) * LANES
                    ]
        return carry

    lax.fori_loop(0, depth // 32, reorder, 0)

    def att_piece(owner, r, hop, target):
        piece = att.at[owner, pl.ds(r * span, span)]
        return pltpu.make_async_remote_copy(
            src_ref=piece,
            dst_ref=piece,
            send_sem=att_send_sem.at[hop, r],
            recv_sem=att_recv_sem.at[owner, r],
            device_id={"tensor": target},
            device_id_type=MESH,
        )

    def join(r, carry):
        sources = [lax.rem(me + i, n_tensor) for i in range(n_tensor)]
        for source in sources[1:]:
            for copy in parts_from(source, r):
                copy.wait_recv()
        stats = [st_send[me, r]] + [st_recv[source, r] for source in sources[1:]]
        peak = functools.reduce(jnp.maximum, [s[0:1] for s in stats])
        factors = [jnp.exp2((s[0:1] - peak) * coef) for s in stats]
        total = sum(s[4:5] * f for s, f in zip(stats, factors))
        summed = o_send[me, r].astype(jnp.float32) * factors[0]
        for source, factor in zip(sources[1:], factors[1:]):
            summed = summed + o_recv[source, r].astype(jnp.float32) * factor
        done = (summed / total).T.astype(jnp.bfloat16)
        for h in range(heads):
            att[me, pl.ds(r * span, span), h * HD : (h + 1) * HD] = done[h * span : (h + 1) * span]
        for d in range(1, chips):
            att_piece(me, r, d, other_chip(d) * 2 + core).start()
        att_piece(me, r, 0, partner).start()
        return carry

    lax.fori_loop(0, requests, join, 0)

    def term(owner, g):
        return jnp.dot(
            att[owner],
            w_ready[g, pl.ds(owner * depth_each, depth_each), :],
            preferred_element_type=jnp.float32,
        )

    def own_term(g, carry):
        acc[g] = term(me, g)
        return carry

    lax.fori_loop(0, col_groups, own_term, 0)

    def relay(r, carry):
        for d in range(1, chips):
            owner = other_chip(d) * 2 + core
            att_piece(owner, r, 0, partner).wait_recv()
            att_piece(owner, r, chips - 1 + d, partner).start()
        return carry

    lax.fori_loop(0, requests, relay, 0)

    def partner_arrives(r, carry):
        att_piece(partner, r, 0, partner).wait_recv()
        return carry

    lax.fori_loop(0, requests, partner_arrives, 0)

    near = [partner] + [other_chip(d) * 2 + core for d in range(1, chips)]

    def near_terms(g, carry):
        acc[g] += sum(term(owner, g) for owner in near)
        return carry

    lax.fori_loop(0, col_groups, near_terms, 0)

    last = [other_chip(d) * 2 + 1 - core for d in range(1, chips)]

    def last_arrives(r, carry):
        for owner in last:
            att_piece(owner, r, 0, partner).wait_recv()
        return carry

    lax.fori_loop(0, requests, last_arrives, 0)

    def share_to(target):
        return pltpu.make_async_remote_copy(
            src_ref=p_send.at[target],
            dst_ref=p_recv.at[me_p],
            send_sem=p_sems.at[0, target],
            recv_sem=p_sems.at[1, me_p],
            device_id={"pipe": target},
            device_id_type=MESH,
        )

    def share_from(source):
        return pltpu.make_async_remote_copy(
            src_ref=p_send.at[source],
            dst_ref=p_recv.at[source],
            send_sem=p_sems.at[0, source],
            recv_sem=p_sems.at[1, source],
            device_id={"pipe": source},
            device_id_type=MESH,
        )

    def finish_share(g):
        p_send[g] = (acc[g] + sum(term(owner, g) for owner in last)).astype(jnp.bfloat16)

    def send_share(i, carry):
        g = lax.rem(me_p + 1 + lax.rem(i + 1, n_pipe - 1), n_pipe)
        finish_share(g)
        share_to(g).start()
        return carry

    lax.fori_loop(0, n_pipe - 1, send_share, 0)
    finish_share(me_p)

    updated = res_ref[...].astype(jnp.float32) + p_send[me_p].astype(jnp.float32)
    for i in (1, 3, 2) if n_pipe == 4 else range(1, n_pipe):
        source = lax.rem(me_p + i, n_pipe)
        share_from(source).wait_recv()
        updated = updated + p_recv[source].astype(jnp.float32)

    mine = jnp.sum(updated * updated, axis=1, keepdims=True)
    sq_send[...] = jnp.broadcast_to(mine, (tokens, LANES)).T[0:8]

    def squares(other, slot_sem, recv_index, recv_slot):
        return pltpu.make_async_remote_copy(
            src_ref=sq_send,
            dst_ref=sq_recv.at[recv_slot],
            send_sem=sq_sems.at[0, slot_sem],
            recv_sem=sq_sems.at[1, recv_index],
            device_id={"pipe": other // n_tensor, "tensor": lax.rem(other, n_tensor)},
            device_id_type=MESH,
        )

    def send_squares(i, carry):
        other = lax.rem(flat + i, devices)
        squares(other, other, flat, flat).start()
        return carry

    lax.fori_loop(1, devices, send_squares, 0)
    residual_out[...] = updated.astype(residual_out.dtype)
    scaled = updated * gain_ref[...]

    def take_squares(i, so_far):
        other = lax.rem(flat + i, devices)
        squares(other, other, other, other).wait_recv()
        return so_far + sq_recv[other]

    all_squares = lax.fori_loop(1, devices, take_squares, sq_send[...])
    mean = all_squares[0:1] / (devices * width)
    factor = jnp.broadcast_to(lax.rsqrt(mean + epsilon), (LANES, tokens)).T[:, 0:1]
    normed_out[...] = (scaled * factor).astype(normed_out.dtype)

    def end_squares(i, carry):
        other = lax.rem(flat + i, devices)
        squares(other, other, other, other).wait_send()
        return carry

    lax.fori_loop(1, devices, end_squares, 0)
    for i in range(1, n_pipe):
        share_to(lax.rem(me_p + i, n_pipe)).wait_send()

    def end_pieces(r, carry):
        for hop in range(2 * chips - 1):
            q_piece(chip, core, r, hop, partner).wait_send()
            att_piece(me, r, hop, partner).wait_send()
        for i in range(1, n_tensor):
            for copy in parts_to(lax.rem(me + i, n_tensor), r):
                copy.wait_send()
        return carry

    lax.fori_loop(0, requests, end_pieces, 0)


def on_device(
    n_pipe,
    n_tensor,
    queries,
    cache_keys,
    cache_values,
    prefix_lengths,
    residual_in,
    out_weight,
    norm_gain,
):
    tokens, columns = queries.shape
    requests, slots, kv_columns = cache_keys.shape
    groups = kv_columns // HD
    depth, col_groups, width = out_weight.shape
    span = tokens // requests
    rows = columns // HD * span
    chips = n_tensor // 2
    blocks = width // LANES
    w = (
        out_weight.reshape(depth, col_groups, blocks, LANES)
        .transpose(0, 2, 1, 3)
        .reshape(depth * blocks * col_groups, LANES)
    )
    bf16, f32 = jnp.bfloat16, jnp.float32
    dma = pltpu.SemaphoreType.DMA
    vmem = pl.BlockSpec(memory_space=pltpu.VMEM)
    hbm = pl.BlockSpec(memory_space=pl.ANY)
    hops = 2 * chips - 1
    out = jax.ShapeDtypeStruct((tokens, width), bf16)
    return pl.pallas_call(
        functools.partial(kernel, n_pipe, n_tensor, requests),
        out_shape=(out, out),
        in_specs=[pl.BlockSpec(memory_space=pltpu.SMEM), hbm, hbm, hbm, hbm, vmem, vmem],
        out_specs=(vmem, vmem),
        scratch_shapes=[
            pltpu.VMEM((chips, requests, 2 * rows, HD), bf16),
            pltpu.VMEM((requests, groups, slots, HD), bf16),
            pltpu.VMEM((requests, groups, slots, HD), bf16),
            pltpu.VMEM(w.shape, bf16),
            pltpu.VMEM((col_groups, depth, width), bf16),
            pltpu.VMEM((n_tensor, requests, HD, rows), bf16),
            pltpu.VMEM((n_tensor, requests, 8, rows), f32),
            pltpu.VMEM((n_tensor, requests, HD, rows), bf16),
            pltpu.VMEM((n_tensor, requests, 8, rows), f32),
            pltpu.VMEM((n_tensor, tokens, columns), bf16),
            pltpu.VMEM((col_groups, tokens, width), f32),
            pltpu.VMEM((n_pipe, tokens, width), bf16),
            pltpu.VMEM((n_pipe, tokens, width), bf16),
            pltpu.VMEM((8, tokens), f32),
            pltpu.VMEM((n_pipe * n_tensor, 8, tokens), f32),
            dma((requests, columns // HD)),
            dma((2, requests, groups)),
            dma,
            dma((hops, requests)),
            dma((n_tensor, requests)),
            dma((2, n_tensor, requests)),
            dma((2, n_tensor, requests)),
            dma((hops, requests)),
            dma((n_tensor, requests)),
            dma((2, n_pipe)),
            dma((2, n_pipe * n_tensor)),
        ],
        compiler_params=pltpu.CompilerParams(
            collective_id=0, has_side_effects=True, vmem_limit_bytes=60 * 1024 * 1024
        ),
    )(
        prefix_lengths,
        queries,
        cache_keys,
        cache_values,
        w,
        residual_in,
        norm_gain.reshape(1, width),
    )


def solution(mesh):
    in_specs = (
        P("replica", ("pipe", "tensor")),
        P("replica", "tensor", "pipe"),
        P("replica", "tensor", "pipe"),
        P("replica"),
        P("replica", ("pipe", "tensor")),
        P("pipe", None, "tensor"),
        P(("pipe", "tensor")),
    )
    out_specs = (P("replica", ("pipe", "tensor")), P("replica", ("pipe", "tensor")))
    return jax.shard_map(
        functools.partial(on_device, mesh.shape["pipe"], mesh.shape["tensor"]),
        mesh=mesh,
        in_specs=in_specs,
        out_specs=out_specs,
        check_vma=False,
    )
```

time: 148 us -> 57.9 us (0.39)
  Pallas kernels: 0 us -> 53.9 us
  blocking collectives: 48.9 us -> 0 us
  local copies, waits for them, and re-layouts: 32.2 us -> 3.14 us
  waiting for transfers between devices: 22.7 us -> 0 us
  other arithmetic: 15.6 us -> 0 us
  between operations: 14.2 us -> 0.64 us
  matrix products: 13 us -> 0 us
    pallas_call x0 -> x1, Pallas kernels: none -> 53.9 us  [on_device(): pl.pallas_call(functools.partial(kernel, n_pipe, n_tensor, requests), out...]
    psum x1 -> x0, blocking collectives: 29.5 us -> none  [on_device(): squares = lax.psum(jnp.sum(updated * updated, axis=1), ('pipe', 'tensor'))]
    reduce_scatter x1 -> x0, waiting for transfers between devices: 22.6 us -> none  [on_device(): lax.psum_scatter(partial_value.reshape(tok_rows, col_groups, col_width).a...]
    all_gather x3 -> x0, blocking collectives: 19.4 us -> none  [the longest x2 10.6 us: combined_all(): lax.all_gather(part.astype(kind), axis)]
    dot_general x3 -> x0, matrix products: 13 us -> none  [the longest x1 7.12 us: on_device(): jnp.dot(attended, out_weight.reshape(out_weight.shape[0], col_groups * co...]
    dot_general x1 -> x0, local copies, waits for them, and re-layouts: 12.3 us -> none  [on_device(): jnp.dot(attended, out_weight.reshape(out_weight.shape[0], col_groups * co...]
    unnamed x8 -> x2, local copies, waits for them, and re-layouts: 11.2 us -> 3.14 us
    reshape x3 -> x0, local copies, waits for them, and re-layouts: 6.74 us -> none  [the longest x1 3.97 us: on_device(): keys_here = cache_keys.reshape(requests, slot_count, local_groups, HD)]
  transfers between devices with their start and end apart: 2 -> 0, of which waited for: 1 -> 0; matrix products, arithmetic and copies ran while one was open for 19% -> 0% of each run, Pallas kernels for 0% -> 0%
where the time goes in v1:
time: 57.9 us; the launch traced here: 57.7 us
  Pallas kernels  53.9 us (93%)
  local copies, waits for them, and re-layouts  3.14 us (5%)
  between operations  0.64 us (1%)
    pallas_call x1, Pallas kernels, on_device(): pl.pallas_call(functools.partial(kernel, n_pipe, n_tensor, requests), out...  53.9 us
    unnamed x2, local copies, waits for them, and re-layouts  3.14 us

profile of v1, /device:TPU:0, one launch (start us, length us, event | category | flops | bytes accessed | tf_op | source)
XLA Modules:
  0.0 57.7 jit_solution(4358837891001035348)
XLA Ops:
  0.6 53.9 %shard_map.86 = (bf16[128,512]{1,0:T(8,128)(2,1)}, bf16[128,512]{1,0:T(8,128)(2,1)}) custom-call(s32[4]{0:T(128)} %prefix_ref.1, bf16[128,512]{1,0:T(8,128)(2,1)} %q_hbm.1, bf16[4,1024,256]{2,1,0:T(8,128)(2,1)} %k_hbm.1, bf16[4,1024,256]{2,1,0:T(8,128)(2,1)} %v_hbm.1, bf16[32768,128]{1,0:T(8,128)(2,1)} %bitcast.6, bf16[128,512]{1,0:T(8,128)(2,1)} %res_ref.1, ...), custom_call_target="tpu_custom_call" | custom-call | tf_op jit(solution)/shard_map/pallas_call | solution.py:468
  54.6 1.6 %copy.12 = bf16[128,512]{1,0:T(8,128)(2,1)} copy(bf16[128,512]{1,0:T(8,128)(2,1)} %get-tuple-element.4) | data formatting | bytes 262144
  56.2 1.6 %copy.13 = bf16[128,512]{1,0:T(8,128)(2,1)} copy(bf16[128,512]{1,0:T(8,128)(2,1)} %get-tuple-element.5) | data formatting | bytes 262144

commit v2 on v1

--- a/solution.py
+++ b/solution.py
@@ -220,6 +220,37 @@
             q_piece(other_chip(d), core, r, chips - 1 + d, partner).start()
         return carry
 
+    lane_blocks = width // LANES
+    per_depth = lane_blocks * col_groups
+    block = 16 * per_depth
+    wide = 4
+    to_row = lax.broadcasted_iota(jnp.int32, (block, block), 0)
+    from_row = lax.broadcasted_iota(jnp.int32, (block, block), 1)
+    order = jnp.where(
+        from_row == lax.rem(to_row, 16) * per_depth + to_row // 16, 1.0, 0.0
+    ).astype(jnp.bfloat16)
+
+    def reorder(i, carry):
+        pair = jnp.concatenate(
+            [w_raw[pl.ds((wide * i + k) * block, block), :] for k in range(wide)], axis=1
+        )
+        ordered = jnp.dot(order, pair, preferred_element_type=jnp.float32).astype(jnp.bfloat16)
+        for j in range(lane_blocks):
+            for g in range(col_groups):
+                at = (j * col_groups + g) * 16
+                for k in range(wide):
+                    w_ready[g, pl.ds((wide * i + k) * 16, 16), j * LANES : (j + 1) * LANES] = ordered[
+                        at : at + 16, k * LANES : (k + 1) * LANES
+                    ]
+        return carry
+
+    def reorder_of(owner):
+        steps = depth_each // (16 * wide)
+        lax.fori_loop(owner * steps, (owner + 1) * steps, reorder, 0)
+
+    w_copy.wait()
+    reorder_of(me)
+
     lax.fori_loop(0, requests, own_unit, 0)
 
     for gi in range(1, n_groups):
@@ -240,31 +271,10 @@
 
     lax.fori_loop(0, (chips - 1) * requests, far_unit, 0)
 
-    w_copy.wait()
-    lane_blocks = width // LANES
-    per_depth = lane_blocks * col_groups
-    block = 16 * per_depth
-    to_row = lax.broadcasted_iota(jnp.int32, (block, block), 0)
-    from_row = lax.broadcasted_iota(jnp.int32, (block, block), 1)
-    order = jnp.where(
-        from_row == lax.rem(to_row, 16) * per_depth + to_row // 16, 1.0, 0.0
-    ).astype(jnp.bfloat16)
-
-    def reorder(i, carry):
-        pair = jnp.concatenate(
-            [w_raw[pl.ds((2 * i + k) * block, block), :] for k in range(2)], axis=1
-        )
-        ordered = jnp.dot(order, pair, preferred_element_type=jnp.float32).astype(jnp.bfloat16)
-        for j in range(lane_blocks):
-            for g in range(col_groups):
-                at = (j * col_groups + g) * 16
-                for k in range(2):
-                    w_ready[g, pl.ds((2 * i + k) * 16, 16), j * LANES : (j + 1) * LANES] = ordered[
-                        at : at + 16, k * LANES : (k + 1) * LANES
-                    ]
-        return carry
-
-    lax.fori_loop(0, depth // 32, reorder, 0)
+    near = [partner] + [other_chip(d) * 2 + core for d in range(1, chips)]
+    last = [other_chip(d) * 2 + 1 - core for d in range(1, chips)]
+    for owner in near:
+        reorder_of(owner)
 
     def att_piece(owner, r, hop, target):
         piece = att.at[owner, pl.ds(r * span, span)]
@@ -311,6 +321,8 @@
         return carry
 
     lax.fori_loop(0, col_groups, own_term, 0)
+    for owner in last:
+        reorder_of(owner)
 
     def relay(r, carry):
         for d in range(1, chips):
@@ -327,15 +339,11 @@
 
     lax.fori_loop(0, requests, partner_arrives, 0)
 
-    near = [partner] + [other_chip(d) * 2 + core for d in range(1, chips)]
-
     def near_terms(g, carry):
         acc[g] += sum(term(owner, g) for owner in near)
         return carry
 
     lax.fori_loop(0, col_groups, near_terms, 0)
-
-    last = [other_chip(d) * 2 + 1 - core for d in range(1, chips)]
 
     def last_arrives(r, carry):
         for owner in last:
@@ -383,7 +391,7 @@
         updated = updated + p_recv[source].astype(jnp.float32)
 
     mine = jnp.sum(updated * updated, axis=1, keepdims=True)
-    sq_send[...] = jnp.broadcast_to(mine, (tokens, LANES)).T[0:8]
+    sq_send[...] = jnp.broadcast_to(mine, (tokens, LANES)).T[0:1]
 
     def squares(other, slot_sem, recv_index, recv_slot):
         return pltpu.make_async_remote_copy(
@@ -410,7 +418,7 @@
         return so_far + sq_recv[other]
 
     all_squares = lax.fori_loop(1, devices, take_squares, sq_send[...])
-    mean = all_squares[0:1] / (devices * width)
+    mean = all_squares / (devices * width)
     factor = jnp.broadcast_to(lax.rsqrt(mean + epsilon), (LANES, tokens)).T[:, 0:1]
     normed_out[...] = (scaled * factor).astype(normed_out.dtype)
 
@@ -484,8 +492,8 @@
             pltpu.VMEM((col_groups, tokens, width), f32),
             pltpu.VMEM((n_pipe, tokens, width), bf16),
             pltpu.VMEM((n_pipe, tokens, width), bf16),
-            pltpu.VMEM((8, tokens), f32),
-            pltpu.VMEM((n_pipe * n_tensor, 8, tokens), f32),
+            pltpu.VMEM((1, tokens), f32),
+            pltpu.VMEM((n_pipe * n_tensor, 1, tokens), f32),
             dma((requests, columns // HD)),
             dma((2, requests, groups)),
             dma,

time: 57.9 us -> 50.3 us (0.87)
  Pallas kernels: 53.9 us -> 46.4 us
    pallas_call x1, Pallas kernels: 53.9 us -> 46.4 us  [on_device(): pl.pallas_call(functools.partial(kernel, n_pipe, n_tensor, requests), out...]
where the time goes in v2:
time: 50.3 us; the launch traced here: 50.1 us
  Pallas kernels  46.4 us (92%)
  local copies, waits for them, and re-layouts  3.14 us (6%)
  between operations  0.64 us (1%)
    pallas_call x1, Pallas kernels, on_device(): pl.pallas_call(functools.partial(kernel, n_pipe, n_tensor, requests), out...  46.4 us
    unnamed x2, local copies, waits for them, and re-layouts  3.14 us

profile of v2, /device:TPU:0, one launch (start us, length us, event | category | flops | bytes accessed | tf_op | source)
XLA Modules:
  0.0 50.1 jit_solution(13909497733369730972)
XLA Ops:
  0.6 46.4 %shard_map.86 = (bf16[128,512]{1,0:T(8,128)(2,1)}, bf16[128,512]{1,0:T(8,128)(2,1)}) custom-call(s32[4]{0:T(128)} %prefix_ref.1, bf16[128,512]{1,0:T(8,128)(2,1)} %q_hbm.1, bf16[4,1024,256]{2,1,0:T(8,128)(2,1)} %k_hbm.1, bf16[4,1024,256]{2,1,0:T(8,128)(2,1)} %v_hbm.1, bf16[32768,128]{1,0:T(8,128)(2,1)} %bitcast.6, bf16[128,512]{1,0:T(8,128)(2,1)} %res_ref.1, ...), custom_call_target="tpu_custom_call" | custom-call | tf_op jit(solution)/shard_map/pallas_call | solution.py:476
  47.0 1.6 %copy.12 = bf16[128,512]{1,0:T(8,128)(2,1)} copy(bf16[128,512]{1,0:T(8,128)(2,1)} %get-tuple-element.4) | data formatting | bytes 262144
  48.6 1.6 %copy.13 = bf16[128,512]{1,0:T(8,128)(2,1)} copy(bf16[128,512]{1,0:T(8,128)(2,1)} %get-tuple-element.5) | data formatting | bytes 262144
